TPU v7x, 32 devices: a whole 2x2x4 slice. The times are simulated.
32 devices in a mesh: grp: 2 (over x), wide: 16 (over z, y, core).
Axes of the slice: x: 2, y: 2, z: 4, core: 2. Of those that a mesh axis runs over, the one named last changes fastest.
Arguments:
- x_pool: bfloat16 [16384, 7168], P(('grp', 'wide')), may hold values from -6 to 6
- token_ids: int32 [4096], P(('grp', 'wide')), may hold values from 0 to 16383, as said below
- cotangent: bfloat16 [4096, 7168], P(('grp', 'wide')), may hold values from -6 to 6
- gate_up: bfloat16 [2, 1024, 7168], P(None, 'wide', 'grp'), may hold values from -0.0625 to 0.0625
- down_weight: bfloat16 [1024, 7168], P('wide', 'grp'), may hold values from -0.1875 to 0.1875
- loss_exponent: int32 [1], replicated, may hold values from 3 to 9
Outputs:
- grad_gate_up: bfloat16 [2, 1024, 7168], P(None, 'wide', 'grp')
- grad_down: bfloat16 [1024, 7168], P('wide', 'grp')
Inputs may be any that keep to these rules, and one draw needn't show every extreme that they name: The 128 ids in aligned block b of token_ids name rows b * 512 to (b + 1) * 512 - 1 of x_pool.
All inputs are finite; a program needn't handle non-finite values.
Results may differ from a plain program's by a relative error of at most 0.014.
Values may be sent and summed in bfloat16 or wider, within the bound.
No kernel may reach another device: no remote copies, remote signals or barrier semaphores. Data moves between devices by JAX's collectives and lax.ppermute only.
A program may use at most 192 MiB of HBM per device.

v0:
```python
import jax
import jax.numpy as jnp
import numpy as np
from jax import lax
from jax.sharding import PartitionSpec as P

BLOCKS = 8


def swapped(value, axis, bit):
    mask = 2**bit
    pairs = [(source, source ^ mask) for source in range(lax.axis_size(axis))]
    return lax.ppermute(value, axis, pairs)


def unscale_of(loss_exponent):
    levels = jnp.arange(16, dtype=jnp.int32)
    powers = jnp.asarray(np.power(0.5, np.arange(16)), dtype=jnp.float32)
    return jnp.sum(jnp.where(levels == loss_exponent[0], powers, jnp.float32(0.0)))


def contract_last(left_side, right_side):
    return lax.dot_general(
        left_side, right_side, (((1,), (1,)), ((), ())), preferred_element_type=jnp.float32
    )


def contract_first(left_side, right_side):
    return lax.dot_general(
        left_side, right_side, (((0,), (0,)), ((), ())), preferred_element_type=jnp.float32
    )


def halve_blocks(gradients, wide_index, low_bits):
    for bit_index in reversed(range(low_bits)):
        half_units = gradients.shape[1] // 2
        lower_half = gradients[:, :half_units]
        upper_half = gradients[:, half_units:]
        own_bit = wide_index >> bit_index & 1
        kept_half = jnp.where(own_bit == 0, lower_half, upper_half)
        sent_half = jnp.where(own_bit == 0, upper_half, lower_half).astype(jnp.bfloat16)
        arrived = swapped(sent_half, "wide", bit_index)
        gradients = kept_half + arrived.astype(jnp.float32)
    return gradients


def per_device(x_pool, token_ids, cotangent, gate_up, down_weight, loss_exponent):
    wide_count = lax.axis_size("wide")
    group_count = wide_count // BLOCKS
    low_bits = group_count.bit_length() - 1
    wide_index = lax.axis_index("wide")
    device_index = lax.axis_index("grp") * wide_count + wide_index
    local_rows = token_ids - device_index * x_pool.shape[0]
    picked = jnp.take(x_pool, local_rows, axis=0)
    stacked = jnp.stack([picked, cotangent])
    token_count = stacked.shape[1]
    model_width = stacked.shape[2]
    weight_tile = jnp.concatenate([gate_up, down_weight[None]], axis=0)
    weight_rows = lax.all_gather(weight_tile, "grp", axis=2, tiled=True)
    for bit_index in range(low_bits):
        partner = swapped(weight_rows, "wide", bit_index)
        own_bit = wide_index >> bit_index & 1
        weight_rows = jnp.where(
            own_bit == 0,
            jnp.concatenate([weight_rows, partner], axis=1),
            jnp.concatenate([partner, weight_rows], axis=1),
        )
    hidden_units = weight_rows.shape[1]
    slot_rows = token_count // group_count
    quarters = stacked.reshape(2, group_count, slot_rows, model_width)
    outgoing = jnp.broadcast_to(quarters[:, None], (2, BLOCKS, group_count, slot_rows, model_width))
    outgoing = outgoing.reshape(2, wide_count * slot_rows, model_width)
    gathered = lax.all_to_all(outgoing, "wide", split_axis=1, concat_axis=1, tiled=True)
    tokens_in = gathered[0]
    tokens_grad = gathered[1]
    unscale = unscale_of(loss_exponent)
    gate_up_rows = weight_rows[:2].reshape(2 * hidden_units, model_width)
    projected = contract_last(tokens_in, gate_up_rows)
    gate_act = projected[:, :hidden_units]
    up_act = projected[:, hidden_units:]
    delta_hidden = unscale * contract_last(tokens_grad, weight_rows[2])
    sigmoid_gate = jax.nn.sigmoid(gate_act)
    hidden = (gate_act * sigmoid_gate * up_act).astype(jnp.bfloat16)
    delta_gate = (
        delta_hidden * up_act * sigmoid_gate * (1.0 + gate_act * (1.0 - sigmoid_gate))
    ).astype(jnp.bfloat16)
    delta_up = (delta_hidden * gate_act * sigmoid_gate).astype(jnp.bfloat16)
    delta_pair = jnp.concatenate([delta_gate, delta_up], axis=1)
    grad_pair = contract_first(delta_pair, tokens_in)
    grad_hidden = unscale * contract_first(hidden, tokens_grad)
    gradients = jnp.concatenate([grad_pair, grad_hidden], axis=0).reshape(
        3, hidden_units, model_width
    )
    gradients = halve_blocks(gradients, wide_index, low_bits)
    gradients = lax.psum_scatter(
        gradients.astype(jnp.bfloat16), "grp", scatter_dimension=2, tiled=True
    ).astype(jnp.float32)
    finished = gradients.astype(jnp.bfloat16)
    return (finished[:2], finished[2])


def solution(mesh):
    in_specs = (
        P(("grp", "wide"), None),
        P(("grp", "wide")),
        P(("grp", "wide"), None),
        P(None, "wide", "grp"),
        P("wide", "grp"),
        P(),
    )
    out_specs = (P(None, "wide", "grp"), P("wide", "grp"))
    return jax.shard_map(
        per_device, mesh=mesh, in_specs=in_specs, out_specs=out_specs, check_vma=False
    )
```

profile of v0, /device:TPU:0, one launch (start us, length us, event | category | flops | bytes accessed | tf_op | source)
XLA Modules:
  0.0 880.1 jit_solution(12923270134924933211)
XLA Ops:
  7.2 0.7 compare_and_fusion
  7.8 0.1 broadcast_in_dim.29
  7.9 7.4 gather_fusion
  15.3 0.2 broadcast_select_fusion
  15.6 1.8 maximum_bitcast_fusion
  17.4 3.8 copy.10
  21.2 17.6 %broadcast_in_dim.34 = bf16[2,8,2,64,7168]{4,0,3,2,1:T(2,128)(2,1)} broadcast(bf16[2,2,64,7168]{3,0,2,1:T(2,128)(2,1)S(1)} %copy.10), dimensions={0,2,3,4} | broadcast | bytes 33030144 | tf_op jit(solution)/shard_map/broadcast_in_dim | solution.py:71
  38.8 0.0 copy-start.2
  38.8 0.0 copy-start.3
  38.8 0.0 copy-start.4
  38.8 7.6 all-to-all-start
  46.4 0.0 all-gather.2.cloned.1.call-start
  46.5 0.0 copy-done.2
  46.5 0.0 copy-done.3
  46.5 1.2 pad_maximum_fusion.1
  47.7 0.0 all-gather.2.cloned.1.call-update
  47.7 0.2 reduce-scatter.2.cloned.1.call-start
  48.0 42.6 %all-gather.2.cloned.1.call-done = bf16[3,64,7168]{2,1,0:T(8,128)(2,1)} async-done(((bf16[3,64,3584]{2,1,0:T(8,128)(2,1)}), bf16[3,64,7168]{2,1,0:T(8,128)(2,1)}) %all-gather.2.cloned.1.call-update) | async-done | bytes 2752528 | tf_op jit(solution)/shard_map/all_gather | solution.py:59
  90.6 0.0 collective-permute-start
  91.2 0.0 copy-done.4
  91.2 0.6 fusion.8
  91.8 4.0 collective-permute-done
  95.9 4.3 maximum_select_fusion
  100.2 0.0 copy-start
  100.2 2.4 copy-done
  102.6 2.2 slice.45
  104.8 457.4 %all-to-all-done = bf16[2,1024,7168]{2,0,1:T(2,128)(2,1)} async-done(((bf16[2,1024,7168]{2,0,1:T(2,128)(2,1)}), bf16[2,1024,7168]{2,0,1:T(2,128)(2,1)}, u32[]{:S(2)}, u32[]{:S(2)}) %all-to-all-start) | async-done | bytes 29360160 | tf_op jit(solution)/shard_map/all_to_all | solution.py:73
  562.2 0.0 copy-start.1
  562.2 55.9 %fusion.11 = (bf16[1,1024,7168]{2,0,1:T(2,128)(2,1)}, bf16[1,1024,7168]{2,0,1:T(2,128)(2,1)}) fusion(bf16[2,1024,7168]{2,0,1:T(2,128)(2,1)} %all-to-all-done), kind=kLoop, calls=%fused_computation.32 | loop fusion | bytes 58720256 | tf_op jit(solution)/shard_map/slice | solution.py:74
  618.1 0.0 copy-done.1
  618.1 18.2 %fusion.2 = f32[1024,256]{0,1:T(8,128)S(1)} fusion(bf16[256,7168]{1,0:T(8,128)(2,1)S(1)} %bitcast.36, bf16[1,1024,7168]{2,0,1:T(2,128)(2,1)} %get-tuple-element.4), kind=kOutput, calls=%fused_computation.7 | convolution fusion | flops 3758096384 | bytes 19398656 | tf_op jit(solution)/shard_map/dot_general | solution.py:23
  636.3 16.1 %multiply_convert_fusion.2 = (bf16[1024,128]{0,1:T(8,128)(2,1)S(1)}, bf16[1024,128]{0,1:T(8,128)(2,1)S(1)}) fusion(f32[1024,256]{0,1:T(8,128)S(1)} %fusion.2, bf16[3,128,7168]{2,1,0:T(8,128)(2,1)} %copy-done, bf16[1,1024,7168]{2,0,1:T(2,128)(2,1)} %get-tuple-element.5, f32[]{:T(128)} %fusion.8), kind=kOutput, calls=%fused_computation.21 | convolution fusion | flops 1880883200 | bytes 32768512 | tf_op jit(solution)/shard_map/dot_general | solution.py:23
  652.4 17.1 %convolution_multiply_fusion = f32[128,7168]{1,0:T(8,128)} fusion(bf16[1,1024,7168]{2,0,1:T(2,128)(2,1)} %get-tuple-element.5, f32[]{:T(128)} %fusion.8, f32[1024,256]{0,1:T(8,128)S(1)} %fusion.2), kind=kOutput, calls=%fused_computation.4 | convolution fusion | flops 1880752128 | bytes 19398660 | tf_op jit(solution)/shard_map/dot_general | solution.py:29
  669.6 17.7 %fusion.1 = f32[256,7168]{1,0:T(8,128)} fusion(bf16[1,1024,7168]{2,0,1:T(2,128)(2,1)} %get-tuple-element.4, bf16[1024,128]{0,1:T(8,128)(2,1)S(1)} %get-tuple-element.7, bf16[1024,128]{0,1:T(8,128)(2,1)S(1)} %get-tuple-element.6), kind=kOutput, calls=%fused_computation.6 | convolution fusion | flops 3759144960 | bytes 22544384 | tf_op jit(solution)/shard_map/dot_general | solution.py:29
  687.3 9.6 %pad_maximum_fusion = f32[384,7168]{1,0:T(8,128)} fusion(f32[128,7168]{1,0:T(8,128)} %convolution_multiply_fusion, f32[256,7168]{1,0:T(8,128)} %fusion.1), kind=kLoop, calls=%fused_computation.3 | loop fusion | flops 2752512 | bytes 22020096 | tf_op jit(solution)/shard_map/concatenate | solution.py:91
  696.9 4.7 select_convert_fusion
  701.6 1.0 collective-permute-start.1
  702.6 4.7 collective-permute-done.1
  707.3 7.1 add_convert_fusion
  714.5 0.0 reduce-scatter.2.cloned.1.call-update
  714.5 154.8 %reduce-scatter.2.cloned.1.call-done = bf16[3,64,3584]{2,1,0:T(8,128)(2,1)} async-done(((bf16[3,64,7168]{2,1,0:T(8,128)(2,1)}), bf16[3,64,3584]{2,1,0:T(8,128)(2,1)}) %reduce-scatter.2.cloned.1.call-update) | async-done | bytes 1376272 | tf_op jit(solution)/shard_map/reduce_scatter | solution.py:95
  869.3 2.2 slice.50
  871.4 1.8 slice_bitcast_fusion.4
  (1 shorter events, 0.0 us)
Async XLA Ops:
  38.8 7.7 copy-start.2
  38.8 7.7 copy-start.3
  38.8 52.4 %copy-start.4 = (f32[16]{0:T(128)S(1)}, f32[16]{0:T(128)}, u32[]{:S(2)}) copy-start(f32[16]{0:T(128)} %constant.37.clone) | copy-start | bytes 196
  38.8 523.3 %all-to-all-start = ((bf16[2,1024,7168]{2,0,1:T(2,128)(2,1)}), bf16[2,1024,7168]{2,0,1:T(2,128)(2,1)}, u32[]{:S(2)}, u32[]{:S(2)}) async-start(bf16[2,1024,7168]{2,0,1:T(2,128)(2,1)} %bitcast.32), calls=%async_computation | async-start | bytes 58720256 | tf_op jit(solution)/shard_map/all_to_all | solution.py:73
  46.4 44.1 %all-gather.2.cloned.1.call-start = ((), (), s32[]{:S(2)}) async-start(), calls=%async_computation.2 | async-start | bytes 4128768 | tf_op jit(solution)/shard_map/all_gather | solution.py:59
  47.7 821.5 %reduce-scatter.2.cloned.1.call-start = ((), (), s32[]{:S(2)}) async-start(), calls=%async_computation.3 | async-start | bytes 4128768 | tf_op jit(solution)/shard_map/reduce_scatter | solution.py:95
  90.6 5.3 collective-permute-start
  100.2 2.4 copy-start
  562.2 55.9 %copy-start.1 = (bf16[2,128,7168]{2,1,0:T(8,128)(2,1)S(1)}, bf16[2,128,7168]{2,1,0:T(8,128)(2,1)}, u32[]{:S(2)}) copy-start(bf16[2,128,7168]{2,1,0:T(8,128)(2,1)} %slice.45) | copy-start | bytes 11010052
  701.6 5.8 collective-permute-start.1
Sparse Core Ops, SparseCore 0:
  48.8 41.7 all-gather.1
  714.6 154.6 reduce-scatter.1
where the time goes:
time: 881 us; the launch traced here: 880 us
  waiting for transfers between devices  664 us (75%)
  local copies, waits for them, and re-layouts  93.3 us (11%)
  matrix products  69.2 us (8%)
  other arithmetic  30.3 us (3%)
  between operations  14.8 us (2%)
  starting transfers between devices  8.9 us (1%)
    all_to_all x1, waiting for transfers between devices, per_device(): lax.all_to_all(outgoing, 'wide', split_axis=1, concat_axis=1, tiled=True)  457 us
    reduce_scatter x1, waiting for transfers between devices, per_device(): lax.psum_scatter(gradients.astype(jnp.bfloat16), 'grp', scatter_dimension...  155 us
    slice x1, local copies, waits for them, and re-layouts, per_device(): tokens_in = gathered[0]  55.9 us
    all_gather x1, waiting for transfers between devices, per_device(): weight_rows = lax.all_gather(weight_tile, 'grp', axis=2, tiled=True)  42.6 us
    dot_general x2, matrix products, contract_first(): lax.dot_general(left_side, right_side, (((0,), (0,)), ((), ())), preferre...  34.8 us
    dot_general x2, matrix products, contract_last(): lax.dot_general(left_side, right_side, (((1,), (1,)), ((), ())), preferre...  34.3 us
    broadcast_in_dim x2, local copies, waits for them, and re-layouts, per_device(): jnp.broadcast_to(quarters[:, None], (2, BLOCKS, group_count, slot_rows, m...  21.4 us
  transfers between devices with their start and end apart: 5, of which 5 were waited for; matrix products, arithmetic and copies ran while one was open for 1% of the time, Pallas kernels for 0%

commit v1 on v0

--- a/solution.py
+++ b/solution.py
@@ -70,7 +70,9 @@
     quarters = stacked.reshape(2, group_count, slot_rows, model_width)
     outgoing = jnp.broadcast_to(quarters[:, None], (2, BLOCKS, group_count, slot_rows, model_width))
     outgoing = outgoing.reshape(2, wide_count * slot_rows, model_width)
-    gathered = lax.all_to_all(outgoing, "wide", split_axis=1, concat_axis=1, tiled=True)
+    shards = jnp.split(outgoing, lax.axis_size("wide"), axis=1)
+    got = lax.all_to_all(jnp.stack(shards), "wide", 0, 0)
+    gathered = jnp.concatenate(got, axis=1)
     tokens_in = gathered[0]
     tokens_grad = gathered[1]
     unscale = unscale_of(loss_exponent)

time: 881 us -> 818 us (0.928)
  matrix products: 69.2 us -> 26 us
  local copies, waits for them, and re-layouts: 93.3 us -> 73.9 us
    slice x1, local copies, waits for them, and re-layouts: 55.9 us -> 11.6 us  [per_device(): tokens_in = gathered[0]]
    unnamed x10 -> x25, local copies, waits for them, and re-layouts: 2.41 us -> 37.4 us
    dot_general x2, matrix products: 34.8 us -> 11.9 us  [contract_first(): lax.dot_general(left_side, right_side, (((0,), (0,)), ((), ())), preferre...]
    dot_general x2, matrix products: 34.3 us -> 14.1 us  [contract_last(): lax.dot_general(left_side, right_side, (((1,), (1,)), ((), ())), preferre...]
    broadcast_in_dim x2 -> x1, local copies, waits for them, and re-layouts: 21.4 us -> 9.98 us  [per_device(): jnp.broadcast_to(quarters[:, None], (2, BLOCKS, group_count, slot_rows, m...]
where the time goes in v1:
time: 818 us
  waiting for transfers between devices  664 us (81%)
  local copies, waits for them, and re-layouts  73.9 us (9%)
  other arithmetic  30.4 us (4%)
  matrix products  26 us (3%)
  between operations  14.8 us (2%)
  starting transfers between devices  8.89 us (1%)
    all_to_all x1, waiting for transfers between devices, per_device(): got = lax.all_to_all(jnp.stack(shards), 'wide', 0, 0)  457 us
    reduce_scatter x1, waiting for transfers between devices, per_device(): lax.psum_scatter(gradients.astype(jnp.bfloat16), 'grp', scatter_dimension...  155 us
    all_gather x1, waiting for transfers between devices, per_device(): weight_rows = lax.all_gather(weight_tile, 'grp', axis=2, tiled=True)  42.6 us
    unnamed x25, local copies, waits for them, and re-layouts  37.4 us
  transfers between devices with their start and end apart: 5, of which 5 were waited for; matrix products, arithmetic and copies ran while one was open for 1% of the time, Pallas kernels for 0%

profile of v1, /device:TPU:0, one launch (start us, length us, event | category | flops | bytes accessed | tf_op | source)
XLA Modules:
  0.0 817.5 jit_solution(906632149908805377)
XLA Ops:
  7.2 0.7 compare_and_fusion
  7.8 0.1 broadcast_in_dim.29
  7.9 7.4 gather_fusion
  15.3 0.2 broadcast_select_fusion
  15.6 1.8 maximum_bitcast_fusion
  17.4 10.0 %broadcast_in_dim.34 = bf16[2,8,2,64,7168]{4,3,2,1,0:T(8,128)(2,1)} broadcast(bf16[2,2,64,7168]{3,2,1,0:T(8,128)(2,1)S(1)} %maximum_bitcast_fusion), dimensions={0,2,3,4} | broadcast | bytes 33030144 | tf_op jit(solution)/shard_map/broadcast_in_dim | solution.py:71
  27.4 0.0 copy-start
  27.4 3.0 fusion.16
  30.4 3.6 fusion.15
  34.1 3.6 fusion.14
  37.6 3.6 fusion.13
  41.2 2.9 fusion.12
  44.1 2.9 fusion.11
  47.0 2.9 fusion.10
  49.9 2.9 fusion.9
  52.8 0.0 copy-done
  52.8 1.3 fusion.8
  54.1 1.4 fusion.7
  55.5 1.3 fusion.6
  56.9 1.4 fusion.5
  58.2 1.4 fusion.4
  59.6 1.4 fusion.3
  61.0 1.3 fusion.2
  62.3 1.4 fusion.1
  63.7 0.0 copy-start.2
  63.7 0.0 copy-start.3
  63.7 0.0 copy-start.4
  63.7 7.6 all-to-all-start
  71.3 0.0 all-gather.2.cloned.1.call-start
  71.4 0.0 copy-done.2
  71.4 0.0 copy-done.3
  71.4 1.2 pad_maximum_fusion.1
  72.6 0.0 all-gather.2.cloned.1.call-update
  72.6 0.2 reduce-scatter.2.cloned.1.call-start
  72.9 42.6 %all-gather.2.cloned.1.call-done = bf16[3,64,7168]{2,1,0:T(8,128)(2,1)} async-done(((bf16[3,64,3584]{2,1,0:T(8,128)(2,1)}), bf16[3,64,7168]{2,1,0:T(8,128)(2,1)}) %all-gather.2.cloned.1.call-update) | async-done | bytes 2752528 | tf_op jit(solution)/shard_map/all_gather | solution.py:59
  115.5 0.0 collective-permute-start
  116.1 0.0 copy-done.4
  116.1 0.7 fusion.23
  116.8 4.0 collective-permute-done
  120.8 4.3 maximum_select_fusion
  125.1 0.0 copy-start.1
  125.1 2.5 copy-done.1
  127.6 2.0 slice.47
  129.6 457.5 %all-to-all-done = bf16[16,2,64,7168]{3,2,1,0:T(8,128)(2,1)} async-done(((bf16[16,2,64,7168]{3,2,1,0:T(8,128)(2,1)}), bf16[16,2,64,7168]{3,2,1,0:T(8,128)(2,1)}, u32[]{:S(2)}, u32[]{:S(2)}) %all-to-all-start) | async-done | bytes 29360160 | tf_op jit(solution)/shard_map/all_to_all | solution.py:74
  587.1 11.6 %fusion.26 = (bf16[1,16,64,7168]{3,2,0,1:T(8,128)(2,1)S(1)}, bf16[1,16,64,7168]{3,2,0,1:T(8,128)(2,1)S(1)}) fusion(bf16[2,16,64,7168]{3,2,0,1:T(8,128)(2,1)} %bitcast.21), kind=kLoop, calls=%fused_computation.61 | loop fusion | bytes 58720256 | tf_op jit(solution)/shard_map/slice | solution.py:76
  598.7 6.0 fusion.27
  604.7 8.1 multiply_convert_fusion.2
  612.8 4.7 convolution_multiply_fusion
  617.5 7.2 fusion.18
  624.7 9.6 %pad_maximum_fusion = f32[384,7168]{1,0:T(8,128)} fusion(f32[128,7168]{1,0:T(8,128)} %convolution_multiply_fusion, f32[256,7168]{1,0:T(8,128)} %fusion.18), kind=kLoop, calls=%fused_computation.1 | loop fusion | flops 2752512 | bytes 22020096 | tf_op jit(solution)/shard_map/concatenate | solution.py:93
  634.3 4.7 select_convert_fusion
  639.0 1.0 collective-permute-start.1
  640.0 4.7 collective-permute-done.1
  644.7 7.1 add_convert_fusion
  651.9 0.0 reduce-scatter.2.cloned.1.call-update
  651.9 154.8 %reduce-scatter.2.cloned.1.call-done = bf16[3,64,3584]{2,1,0:T(8,128)(2,1)} async-done(((bf16[3,64,7168]{2,1,0:T(8,128)(2,1)}), bf16[3,64,3584]{2,1,0:T(8,128)(2,1)}) %reduce-scatter.2.cloned.1.call-update) | async-done | bytes 1376272 | tf_op jit(solution)/shard_map/reduce_scatter | solution.py:97
  806.7 2.2 slice.52
  808.8 1.8 slice_bitcast_fusion.20
  (1 shorter events, 0.0 us)
Async XLA Ops:
  27.4 25.4 %copy-start = (bf16[2,8,2,64,7168]{4,3,2,1,0:T(8,128)(2,1)S(1)}, bf16[2,8,2,64,7168]{4,3,2,1,0:T(8,128)(2,1)}, u32[]{:S(2)}) copy-start(bf16[2,8,2,64,7168]{4,3,2,1,0:T(8,128)(2,1)} %broadcast_in_dim.34) | copy-start | bytes 88080384
  63.7 7.7 copy-start.2
  63.7 7.7 copy-start.3
  63.7 52.4 %copy-start.4 = (f32[16]{0:T(128)S(1)}, f32[16]{0:T(128)}, u32[]{:S(2)}) copy-start(f32[16]{0:T(128)} %constant.37.clone) | copy-start | bytes 196
  63.7 523.3 %all-to-all-start = ((bf16[16,2,64,7168]{3,2,1,0:T(8,128)(2,1)}), bf16[16,2,64,7168]{3,2,1,0:T(8,128)(2,1)}, u32[]{:S(2)}, u32[]{:S(2)}) async-start(bf16[16,2,64,7168]{3,2,1,0:T(8,128)(2,1)} %fusion.1), calls=%async_computation | async-start | bytes 58720256 | tf_op jit(solution)/shard_map/all_to_all | solution.py:74
  71.3 44.1 %all-gather.2.cloned.1.call-start = ((), (), s32[]{:S(2)}) async-start(), calls=%async_computation.2 | async-start | bytes 4128768 | tf_op jit(solution)/shard_map/all_gather | solution.py:59
  72.6 734.1 %reduce-scatter.2.cloned.1.call-start = ((), (), s32[]{:S(2)}) async-start(), calls=%async_computation.3 | async-start | bytes 4128768 | tf_op jit(solution)/shard_map/reduce_scatter | solution.py:97
  115.5 5.3 collective-permute-start
  125.1 2.5 copy-start.1
  639.0 5.8 collective-permute-start.1
Sparse Core Ops, SparseCore 0:
  73.7 41.7 all-gather.1
  652.0 154.6 reduce-scatter.1
